TPU v7x, 32 devices: a whole 2x2x4 slice. The times are simulated.
32 devices in a mesh: gx: 4 (over y, x), gy: 8 (over z, core).
Axes of the slice: x: 2, y: 2, z: 4, core: 2. Of those that a mesh axis runs over, the one named last changes fastest.
Arguments:
- right_side: float32 [128, 2048], P('gx', 'gy'), may hold values from -200 to 200
- reaction: float32 [128, 2048], P('gx', 'gy'), may hold values from 2 to 4
- kernel: float32 [65, 65], replicated, may hold values from -0.04 to 0.04
Outputs:
- solution: float32 [128, 2048], P('gx', 'gy')
- residual: float32 [128, 2048], P('gx', 'gy')
All inputs are finite; a program needn't handle non-finite values.
Results may differ from a plain program's by a relative error of at most 0.00075.
Values sent between devices are 32-bit elements; how exact they have to be, the bound alone decides.
A program may use at most 64 MiB of HBM per device.

v0:
```python
import jax
import jax.numpy as jnp
from jax import lax
from jax.sharding import PartitionSpec as P

ITERS = 4
small_term = 1e-06


def extended(block, sides, width):
    for axis, dim in sides:
        count = lax.axis_size(axis)
        forward = [(i, i + 1) for i in range(count - 1)]
        backward = [(target, source) for source, target in forward]
        low = lax.ppermute(
            lax.slice_in_dim(block, block.shape[dim] - width, None, axis=dim), axis, forward
        )
        high = lax.ppermute(lax.slice_in_dim(block, 0, width, axis=dim), axis, backward)
        block = jnp.concatenate([low, block, high], axis=dim)
    return block


def solve_small(normal_matrix, target, count):
    factor = jnp.linalg.cholesky(normal_matrix)
    forward = []
    for position in range(count):
        accum = target[position]
        for earlier in range(position):
            accum = accum - factor[position, earlier] * forward[earlier]
        forward.append(accum / factor[position, position])
    backward = [None] * count
    for position in reversed(range(count)):
        accum = forward[position]
        for later in range(position + 1, count):
            accum = accum - factor[later, position] * backward[later]
        backward[position] = accum / factor[position, position]
    return backward


def total_norm(values):
    return jnp.sqrt(lax.psum(jnp.sum(values * values), ("gx", "gy")) + small_term)


def local(right_side, reaction, kernel):
    tile_rows, tile_cols = right_side.shape
    kernel_width = kernel.shape[0]
    radius = kernel_width // 2
    bundle = 5
    span_rows = tile_rows + 2 * radius
    period = 2 * tile_rows + 2 * radius
    highest = lax.Precision.HIGHEST

    def extend(values):
        return extended(values, (("gx", 0), ("gy", 1)), radius)

    def apply_operator(values):
        padded = extend(values)

        def group_step(group, summed):
            first_col = group * bundle
            chosen = lax.dynamic_slice_in_dim(kernel, first_col, bundle, 1)
            columns_rev = jnp.pad(chosen[::-1, :].T, ((0, 0), (0, period - kernel_width)))
            toeplitz = jnp.tile(columns_rev, (1, tile_rows))[:, : tile_rows * (period - 1)]
            toeplitz = toeplitz.reshape(bundle, tile_rows, period - 1)[:, :, :span_rows]
            for member in range(bundle):
                offset = 2 * radius - first_col - member
                shifted = lax.dynamic_slice_in_dim(padded, offset, tile_cols, 1)
                summed = summed + jnp.dot(
                    toeplitz[member], shifted, precision=highest, preferred_element_type=jnp.float32
                )
            return summed

        convolved = lax.fori_loop(
            0, kernel_width // bundle, group_step, jnp.zeros((tile_rows, tile_cols), jnp.float32)
        )
        return reaction * values - convolved

    initial_norm = total_norm(right_side)
    krylov = [right_side / initial_norm]
    upper = jnp.zeros((ITERS + 1, ITERS), jnp.float32)
    for column in range(ITERS):
        candidate = apply_operator(krylov[column])
        basis_now = jnp.stack(krylov)
        first_terms = jnp.einsum("kij,ij->k", basis_now, candidate, precision=highest)
        first_terms = lax.psum(first_terms, ("gx", "gy"))
        candidate = candidate - jnp.einsum("k,kij->ij", first_terms, basis_now, precision=highest)
        upper = upper.at[: column + 1, column].set(first_terms)
        length = total_norm(candidate)
        upper = upper.at[column + 1, column].set(length)
        krylov.append(candidate / length)
    normal_matrix = jnp.dot(upper.T, upper, precision=highest)
    coeffs = solve_small(normal_matrix, initial_norm * upper[0, :], ITERS)
    solution = coeffs[0] * krylov[0]
    for column in range(1, ITERS):
        solution = solution + coeffs[column] * krylov[column]
    residual = right_side - apply_operator(solution)
    return (solution, residual)


def solution(mesh):
    in_specs = (P("gx", "gy"), P("gx", "gy"), P())
    out_specs = (P("gx", "gy"), P("gx", "gy"))
    return jax.shard_map(local, mesh=mesh, in_specs=in_specs, out_specs=out_specs, check_vma=False)
```

profile of v0, /device:TPU:3, one launch (start us, length us, event | category | flops | bytes accessed | tf_op | source)
XLA Modules:
  0.0 615.0 jit_solution(7024932952548193070)
XLA Ops:
  2.1 39.9 %psum.63 = f32[]{:T(128)} all-reduce(f32[]{:T(128)} %multiply_reduce_fusion.4), channel_id=1, replica_groups=mesh['gx'=4,'gy'=8] {'gx','gy'}, use_global_device_ids=true, to_apply=%region_1.0 | all-reduce | flops 1 | bytes 8 | tf_op jit(solution)/shard_map/psum | solution.py:41
  42.7 3.1 collective-permute-start
  45.8 2.2 collective-permute-start.1
  51.5 6.8 %collective-permute-start.2 = (f32[96,32]{1,0:T(8,128)S(1)}, f32[96,32]{1,0:T(8,128)S(1)}, u32[]{:S(2)}, u32[]{:S(2)}) collective-permute-start(f32[96,32]{1,0:T(8,128)S(1)} %get-tuple-element.973), channel_id=1, source_target_pairs={{0,1},{1,2},{2,3},{3,4},{4,5},{5,6},{6,7},{8,9},{9,10},{10,11},{11... | collective-permute-start | bytes 36872 | tf_op jit(solution)/shard_map/ppermute | solution.py:15
  63.9 24.5 %while.98 = (s32[]{:T(128)}, f32[32,256]{1,0:T(8,128)S(1)}, f32[65,65]{1,0:T(8,128)S(1)}, f32[96,320]{1,0:T(8,128)S(1)}, s32[]{:T(128)}, /*index=5*/s32[]{:T(128...) while((s32[]{:T(128)}, f32[32,256]{1,0:T(8,128)S(1)}, ...), condition=%wide.region_3.4_spmd.clone, body=%wide.region_2.3_spmd.clone.sunk | while | flops 47235088 | bytes 1324147 | solution.py:73
  89.1 38.0 %psum.64 = f32[1]{0:T(128)} all-reduce(f32[1]{0:T(128)} %bitcast), channel_id=1, replica_groups=mesh['gx'=4,'gy'=8] {'gx','gy'}, use_global_device_ids=true, to_apply=%region_4.5 | all-reduce | flops 1 | bytes 8 | tf_op jit(solution)/shard_map/psum | solution.py:85
  128.4 40.4 %psum.65 = f32[]{:T(128)} all-reduce(f32[]{:T(128)} %get-tuple-element.963), channel_id=1, replica_groups=mesh['gx'=4,'gy'=8] {'gx','gy'}, use_global_device_ids=true, to_apply=%region_6.7 | all-reduce | flops 1 | bytes 8 | tf_op jit(solution)/shard_map/psum | solution.py:41
  169.4 3.1 collective-permute-start.4
  172.5 2.2 collective-permute-start.5
  174.8 3.3 collective-permute-done.5
  178.2 6.0 collective-permute-start.6
  186.1 3.5 collective-permute-done.7
  189.7 24.5 %while.99 = (s32[]{:T(128)}, f32[32,256]{1,0:T(8,128)S(1)}, f32[65,65]{1,0:T(8,128)S(1)}, f32[96,320]{1,0:T(8,128)S(1)}, s32[]{:T(128)}, /*index=5*/s32[]{:T(128...) while((s32[]{:T(128)}, f32[32,256]{1,0:T(8,128)S(1)}, ...), condition=%wide.region_9.10_spmd.clone, body=%wide.region_8.9_spmd.clone.sunk | while | flops 47235088 | bytes 1324147 | solution.py:73
  215.5 37.4 %psum.66 = f32[2]{0:T(128)S(1)} all-reduce(f32[2]{0:T(128)S(1)} %convolution_bitcast_fusion.2), channel_id=1, replica_groups=mesh['gx'=4,'gy'=8] {'gx','gy'}, use_global_device_ids=true, to_apply=%region_10.11 | all-reduce | flops 2 | bytes 16 | tf_op jit(solution)/shard_map/psum | solution.py:85
  254.0 40.5 %psum.67 = f32[]{:T(128)} all-reduce(f32[]{:T(128)} %multiply_reduce_fusion.2), channel_id=1, replica_groups=mesh['gx'=4,'gy'=8] {'gx','gy'}, use_global_device_ids=true, to_apply=%region_12.13 | all-reduce | flops 1 | bytes 8 | tf_op jit(solution)/shard_map/psum | solution.py:41
  295.2 3.1 collective-permute-start.8
  304.0 5.8 collective-permute-start.10
  311.7 3.5 collective-permute-done.11
  315.3 24.5 %while.100 = (s32[]{:T(128)}, f32[32,256]{1,0:T(8,128)S(1)}, f32[65,65]{1,0:T(8,128)S(1)}, f32[96,320]{1,0:T(8,128)S(1)}, s32[]{:T(128)}, /*index=5*/s32[]{:T(12...) while((s32[]{:T(128)}, f32[32,256]{1,0:T(8,128)S(1)}, ...), condition=%wide.region_15.16_spmd.clone, body=%wide.region_14.15_spmd.clone.sunk | while | flops 47235088 | bytes 1324147 | solution.py:73
  341.9 37.4 %psum.68 = f32[3]{0:T(128)S(1)} all-reduce(f32[3]{0:T(128)S(1)} %convolution_bitcast_fusion.1), channel_id=1, replica_groups=mesh['gx'=4,'gy'=8] {'gx','gy'}, use_global_device_ids=true, to_apply=%region_16.17 | all-reduce | flops 3 | bytes 24 | tf_op jit(solution)/shard_map/psum | solution.py:85
  380.4 40.5 %psum.69 = f32[]{:T(128)} all-reduce(f32[]{:T(128)} %multiply_reduce_fusion.1), channel_id=1, replica_groups=mesh['gx'=4,'gy'=8] {'gx','gy'}, use_global_device_ids=true, to_apply=%region_18.19 | all-reduce | flops 1 | bytes 8 | tf_op jit(solution)/shard_map/psum | solution.py:41
  421.7 3.1 collective-permute-start.12
  430.4 5.8 collective-permute-start.14
  438.3 3.3 collective-permute-done.15
  441.7 24.5 %while.101 = (s32[]{:T(128)}, f32[32,256]{1,0:T(8,128)S(1)}, f32[65,65]{1,0:T(8,128)S(1)}, f32[96,320]{1,0:T(8,128)S(1)}, s32[]{:T(128)}, /*index=5*/s32[]{:T(12...) while((s32[]{:T(128)}, f32[32,256]{1,0:T(8,128)S(1)}, ...), condition=%wide.region_21.22_spmd.clone, body=%wide.region_20.21_spmd.clone.sunk | while | flops 47235088 | bytes 1324147 | solution.py:73
  468.2 37.4 %psum.70 = f32[4]{0:T(128)S(1)} all-reduce(f32[4]{0:T(128)S(1)} %convolution_bitcast_fusion), channel_id=1, replica_groups=mesh['gx'=4,'gy'=8] {'gx','gy'}, use_global_device_ids=true, to_apply=%region_22.23 | all-reduce | flops 4 | bytes 32 | tf_op jit(solution)/shard_map/psum | solution.py:85
  506.8 40.5 %psum.71 = f32[]{:T(128)} all-reduce(f32[]{:T(128)} %fusion.60), channel_id=1, replica_groups=mesh['gx'=4,'gy'=8] {'gx','gy'}, use_global_device_ids=true, to_apply=%region_24.25 | all-reduce | flops 1 | bytes 8 | tf_op jit(solution)/shard_map/psum | solution.py:41
  569.8 3.1 collective-permute-start.16
  575.1 3.4 collective-permute-done.17
  578.6 5.8 collective-permute-start.18
  586.3 3.5 collective-permute-done.19
  589.9 24.5 %while.102 = (s32[]{:T(128)}, f32[32,256]{1,0:T(8,128)S(1)}, f32[65,65]{1,0:T(8,128)S(1)}, f32[96,320]{1,0:T(8,128)S(1)}, s32[]{:T(128)}, /*index=5*/s32[]{:T(12...) while((s32[]{:T(128)}, f32[32,256]{1,0:T(8,128)S(1)}, ...), condition=%wide.region_28.29_spmd.clone, body=%wide.region_27.28_spmd.clone.sunk | while | flops 47235088 | bytes 1324147 | solution.py:73
  (890 shorter events, 163.8 us)
Async XLA Ops:
  0.6 42.1 %copy-start.1 = (f32[32,256]{1,0:T(8,128)S(1)}, f32[32,256]{1,0:T(8,128)}, u32[]{:S(2)}) copy-start(f32[32,256]{1,0:T(8,128)} %param.29) | copy-start | bytes 98308
  42.7 7.9 %collective-permute-start = (f32[32,256]{1,0:T(8,128)S(1)}, f32[32,256]{1,0:T(8,128)S(1)}, u32[]{:S(2)}, u32[]{:S(2)}) collective-permute-start(f32[32,256]{1,0:T(8,128)S(1)} %broadcast_divide_fusion.3), channel_id=1, source_target_pairs={{0,8},{8,16},{16,24},{1,9},{9,17},{17,25},{2,10},{10,18},{18,26},{... | collective-permute-start | bytes 98312 | tf_op jit(solution)/shard_map/ppermute | solution.py:15
  45.8 5.6 collective-permute-start.1
  48.7 0.7 copy-start.5
  49.3 0.7 copy-start.4
  51.5 10.1 %collective-permute-start.2 = (f32[96,32]{1,0:T(8,128)S(1)}, f32[96,32]{1,0:T(8,128)S(1)}, u32[]{:S(2)}, u32[]{:S(2)}) collective-permute-start(f32[96,32]{1,0:T(8,128)S(1)} %get-tuple-element.973), channel_id=1, source_target_pairs={{0,1},{1,2},{2,3},{3,4},{4,5},{5,6},{6,7},{8,9},{9,10},{10,11},{11... | collective-permute-start | bytes 36872 | tf_op jit(solution)/shard_map/ppermute | solution.py:15
  58.3 5.4 collective-permute-start.3
  61.6 2.3 copy-start
  63.9 24.5 %copy-start.2 = (f32[32,256]{1,0:T(8,128)S(1)}, f32[32,256]{1,0:T(8,128)}, u32[]{:S(2)}) copy-start(f32[32,256]{1,0:T(8,128)} %param.30) | copy-start | bytes 98308
  169.4 5.3 collective-permute-start.4
  172.5 5.6 collective-permute-start.5
  178.2 7.9 %collective-permute-start.6 = (f32[96,32]{1,0:T(8,128)S(1)}, f32[96,32]{1,0:T(8,128)S(1)}, u32[]{:S(2)}, u32[]{:S(2)}) collective-permute-start(f32[96,32]{1,0:T(8,128)S(1)} %get-tuple-element.971), channel_id=1, source_target_pairs={{0,1},{1,2},{2,3},{3,4},{4,5},{5,6},{6,7},{8,9},{9,10},{10,11},{11... | collective-permute-start | bytes 36872 | tf_op jit(solution)/shard_map/ppermute | solution.py:15
  184.1 5.4 collective-permute-start.7
  295.2 7.2 %collective-permute-start.8 = (f32[32,256]{1,0:T(8,128)S(1)}, f32[32,256]{1,0:T(8,128)S(1)}, u32[]{:S(2)}, u32[]{:S(2)}) collective-permute-start(f32[32,256]{1,0:T(8,128)S(1)} %broadcast_divide_fusion.1), channel_id=1, source_target_pairs={{0,8},{8,16},{16,24},{1,9},{9,17},{17,25},{2,10},{10,18},{18,26},{... | collective-permute-start | bytes 98312 | tf_op jit(solution)/shard_map/ppermute | solution.py:15
  298.3 5.6 collective-permute-start.9
  304.0 7.7 %collective-permute-start.10 = (f32[96,32]{1,0:T(8,128)S(1)}, f32[96,32]{1,0:T(8,128)S(1)}, u32[]{:S(2)}, u32[]{:S(2)}) collective-permute-start(f32[96,32]{1,0:T(8,128)S(1)} %get-tuple-element.969), channel_id=1, source_target_pairs={{0,1},{1,2},{2,3},{3,4},{4,5},{5,6},{6,7},{8,9},{9,10},{10,11},{11... | collective-permute-start | bytes 36872 | tf_op jit(solution)/shard_map/ppermute | solution.py:15
  309.8 5.4 collective-permute-start.11
  421.7 7.1 %collective-permute-start.12 = (f32[32,256]{1,0:T(8,128)S(1)}, f32[32,256]{1,0:T(8,128)S(1)}, u32[]{:S(2)}, u32[]{:S(2)}) collective-permute-start(f32[32,256]{1,0:T(8,128)S(1)} %broadcast_divide_fusion), channel_id=1, source_target_pairs={{0,8},{8,16},{16,24},{1,9},{9,17},{17,25},{2,10},{10,18},{18,26},{... | collective-permute-start | bytes 98312 | tf_op jit(solution)/shard_map/ppermute | solution.py:15
  424.8 5.6 collective-permute-start.13
  430.4 7.9 %collective-permute-start.14 = (f32[96,32]{1,0:T(8,128)S(1)}, f32[96,32]{1,0:T(8,128)S(1)}, u32[]{:S(2)}, u32[]{:S(2)}) collective-permute-start(f32[96,32]{1,0:T(8,128)S(1)} %get-tuple-element.967), channel_id=1, source_target_pairs={{0,1},{1,2},{2,3},{3,4},{4,5},{5,6},{6,7},{8,9},{9,10},{10,11},{11... | collective-permute-start | bytes 36872 | tf_op jit(solution)/shard_map/ppermute | solution.py:15
  436.2 5.4 collective-permute-start.15
  569.8 44.5 %copy-start.3 = (f32[32,256]{1,0:T(8,128)}, f32[32,256]{1,0:T(8,128)S(1)}, u32[]{:S(2)}) copy-start(f32[32,256]{1,0:T(8,128)S(1)} %multiply_add_fusion) | copy-start | bytes 98308
  569.8 5.3 collective-permute-start.16
  572.9 5.6 collective-permute-start.17
  578.6 7.7 %collective-permute-start.18 = (f32[96,32]{1,0:T(8,128)S(1)}, f32[96,32]{1,0:T(8,128)S(1)}, u32[]{:S(2)}, u32[]{:S(2)}) collective-permute-start(f32[96,32]{1,0:T(8,128)S(1)} %get-tuple-element.965), channel_id=1, source_target_pairs={{0,1},{1,2},{2,3},{3,4},{4,5},{5,6},{6,7},{8,9},{9,10},{10,11},{11... | collective-permute-start | bytes 36872 | tf_op jit(solution)/shard_map/ppermute | solution.py:15
  584.4 5.4 collective-permute-start.19
where the time goes:
time: 618 us; the launch traced here: 615 us
  blocking collectives  352 us (57%)
  matrix products  87.7 us (14%)
  starting transfers between devices  66.3 us (11%)
  local copies, waits for them, and re-layouts  37.8 us (6%)
  waiting for transfers between devices  26.2 us (4%)
  between operations  19.8 us (3%)
  other arithmetic  16.1 us (3%)
  loops' own time  8.91 us (1%)
    psum x5, blocking collectives, total_norm(): lax.psum(jnp.sum(values * values), ('gx', 'gy')) + small_term  202 us
    psum x4, blocking collectives, local(): first_terms = lax.psum(first_terms, ('gx', 'gy'))  150 us
    dot_general x325, matrix products, group_step(): jnp.dot(toeplitz[member], shifted, precision=highest, preferred_element_t...  84.5 us
    ppermute x10, starting transfers between devices, extended(): lax.ppermute(lax.slice_in_dim(block, block.shape[dim] - width, None, axis...  45.6 us
    ppermute x10, waiting for transfers between devices, extended(): lax.ppermute(lax.slice_in_dim(block, 0, width, axis=dim), axis, backward)  26.2 us
    ppermute x10, starting transfers between devices, extended(): lax.ppermute(lax.slice_in_dim(block, 0, width, axis=dim), axis, backward)  20.7 us
    reshape x65, local copies, waits for them, and re-layouts, group_step(): toeplitz = toeplitz.reshape(bundle, tile_rows, period - 1)[:, :, :span_rows]  12.6 us
  transfers between devices with their start and end apart: 20, of which 10 were waited for; matrix products, arithmetic and copies ran while one was open for 1% of the time, Pallas kernels for 0%

commit v1 on v0

--- a/solution.py
+++ b/solution.py
@@ -82,7 +82,7 @@
         candidate = apply_operator(krylov[column])
         basis_now = jnp.stack(krylov)
         first_terms = jnp.einsum("kij,ij->k", basis_now, candidate, precision=highest)
-        first_terms = lax.psum(first_terms, ("gx", "gy"))
+        first_terms = lax.psum(lax.psum(first_terms, "gy"), "gx")
         candidate = candidate - jnp.einsum("k,kij->ij", first_terms, basis_now, precision=highest)
         upper = upper.at[: column + 1, column].set(first_terms)
         length = total_norm(candidate)

time: 618 us -> 552 us (0.89)
  blocking collectives: 352 us -> 280 us
    psum x4 -> x8, blocking collectives: 150 us -> 66.7 us  [local(): first_terms = lax.psum(lax.psum(first_terms, 'gy'), 'gx')]
    psum x5, blocking collectives: 202 us -> 213 us  [total_norm(): lax.psum(jnp.sum(values * values), ('gx', 'gy')) + small_term]
  transfers between devices with their start and end apart: 20 -> 20, of which waited for: 10 -> 9; matrix products, arithmetic and copies ran while one was open for 1% -> 1% of each run, Pallas kernels for 0% -> 0%
where the time goes in v1:
time: 552 us; the launch traced here: 550 us
  blocking collectives  280 us (51%)
  matrix products  87.7 us (16%)
  starting transfers between devices  71.9 us (13%)
  local copies, waits for them, and re-layouts  37.8 us (7%)
  waiting for transfers between devices  28.1 us (5%)
  between operations  19.9 us (4%)
  other arithmetic  16 us (3%)
  loops' own time  8.9 us (2%)
    psum x5, blocking collectives, total_norm(): lax.psum(jnp.sum(values * values), ('gx', 'gy')) + small_term  213 us
    dot_general x325, matrix products, group_step(): jnp.dot(toeplitz[member], shifted, precision=highest, preferred_element_t...  84.5 us
    psum x8, blocking collectives, local(): first_terms = lax.psum(lax.psum(first_terms, 'gy'), 'gx')  66.7 us
    ppermute x10, starting transfers between devices, extended(): lax.ppermute(lax.slice_in_dim(block, block.shape[dim] - width, None, axis...  51.4 us
    ppermute x10, waiting for transfers between devices, extended(): lax.ppermute(lax.slice_in_dim(block, 0, width, axis=dim), axis, backward)  28.1 us
    ppermute x10, starting transfers between devices, extended(): lax.ppermute(lax.slice_in_dim(block, 0, width, axis=dim), axis, backward)  20.5 us
    reshape x65, local copies, waits for them, and re-layouts, group_step(): toeplitz = toeplitz.reshape(bundle, tile_rows, period - 1)[:, :, :span_rows]  12.6 us
  transfers between devices with their start and end apart: 20, of which 9 were waited for; matrix products, arithmetic and copies ran while one was open for 1% of the time, Pallas kernels for 0%

profile of v1, /device:TPU:3, one launch (start us, length us, event | category | flops | bytes accessed | tf_op | source)
XLA Modules:
  0.0 550.2 jit_solution(3730955331381555176)
XLA Ops:
  2.1 39.9 %psum.91 = f32[]{:T(128)} all-reduce(f32[]{:T(128)} %multiply_reduce_fusion.4), channel_id=1, replica_groups=mesh['gx'=4,'gy'=8] {'gx','gy'}, use_global_device_ids=true, to_apply=%region_1.0 | all-reduce | flops 1 | bytes 8 | tf_op jit(solution)/shard_map/psum | solution.py:41
  42.7 3.1 collective-permute-start
  51.5 6.8 %collective-permute-start.2 = (f32[96,32]{1,0:T(8,128)S(1)}, f32[96,32]{1,0:T(8,128)S(1)}, u32[]{:S(2)}, u32[]{:S(2)}) collective-permute-start(f32[96,32]{1,0:T(8,128)S(1)} %get-tuple-element.973), channel_id=1, source_target_pairs={{0,1},{1,2},{2,3},{3,4},{4,5},{5,6},{6,7},{8,9},{9,10},{10,11},{11... | collective-permute-start | bytes 36872 | tf_op jit(solution)/shard_map/ppermute | solution.py:15
  63.9 24.5 %while.98 = (s32[]{:T(128)}, f32[32,256]{1,0:T(8,128)S(1)}, f32[65,65]{1,0:T(8,128)S(1)}, f32[96,320]{1,0:T(8,128)S(1)}, s32[]{:T(128)}, /*index=5*/s32[]{:T(128...) while((s32[]{:T(128)}, f32[32,256]{1,0:T(8,128)S(1)}, ...), condition=%wide.region_3.4_spmd.clone, body=%wide.region_2.3_spmd.clone.sunk | while | flops 47235088 | bytes 1324147 | solution.py:73
  89.0 11.3 %psum.92 = f32[1]{0:T(128)} all-reduce(f32[1]{0:T(128)} %bitcast), channel_id=1, replica_groups=mesh['gx'=4,'gy'=8] {'gy'}, use_global_device_ids=true, to_apply=%region_4.5 | all-reduce | flops 1 | bytes 8 | tf_op jit(solution)/shard_map/psum | solution.py:85
  100.3 6.1 %psum.93 = f32[1]{0:T(128)} all-reduce(f32[1]{0:T(128)} %psum.92), channel_id=1, replica_groups=mesh['gx'=4,'gy'=8] {'gx'}, use_global_device_ids=true, to_apply=%region_5.6 | all-reduce | flops 1 | bytes 8 | tf_op jit(solution)/shard_map/psum | solution.py:85
  107.7 43.5 %psum.94 = f32[]{:T(128)} all-reduce(f32[]{:T(128)} %get-tuple-element.963), channel_id=1, replica_groups=mesh['gx'=4,'gy'=8] {'gx','gy'}, use_global_device_ids=true, to_apply=%region_7.8 | all-reduce | flops 1 | bytes 8 | tf_op jit(solution)/shard_map/psum | solution.py:41
  151.9 3.1 collective-permute-start.4
  157.2 3.3 collective-permute-done.5
  160.7 7.3 %collective-permute-start.6 = (f32[96,32]{1,0:T(8,128)S(1)}, f32[96,32]{1,0:T(8,128)S(1)}, u32[]{:S(2)}, u32[]{:S(2)}) collective-permute-start(f32[96,32]{1,0:T(8,128)S(1)} %get-tuple-element.971), channel_id=1, source_target_pairs={{0,1},{1,2},{2,3},{3,4},{4,5},{5,6},{6,7},{8,9},{9,10},{10,11},{11... | collective-permute-start | bytes 36872 | tf_op jit(solution)/shard_map/ppermute | solution.py:15
  169.9 3.5 collective-permute-done.7
  173.5 24.5 %while.99 = (s32[]{:T(128)}, f32[32,256]{1,0:T(8,128)S(1)}, f32[65,65]{1,0:T(8,128)S(1)}, f32[96,320]{1,0:T(8,128)S(1)}, s32[]{:T(128)}, /*index=5*/s32[]{:T(128...) while((s32[]{:T(128)}, f32[32,256]{1,0:T(8,128)S(1)}, ...), condition=%wide.region_10.11_spmd.clone, body=%wide.region_9.10_spmd.clone.sunk | while | flops 47235088 | bytes 1324147 | solution.py:73
  198.6 10.7 %psum.95 = f32[2]{0:T(128)S(1)} all-reduce(f32[2]{0:T(128)S(1)} %convolution_bitcast_fusion.2), channel_id=1, replica_groups=mesh['gx'=4,'gy'=8] {'gy'}, use_global_device_ids=true, to_apply=%region_11.12 | all-reduce | flops 2 | bytes 16 | tf_op jit(solution)/shard_map/psum | solution.py:85
  210.0 5.5 psum.96
  216.4 43.4 %psum.97 = f32[]{:T(128)} all-reduce(f32[]{:T(128)} %multiply_reduce_fusion.2), channel_id=1, replica_groups=mesh['gx'=4,'gy'=8] {'gx','gy'}, use_global_device_ids=true, to_apply=%region_14.15 | all-reduce | flops 1 | bytes 8 | tf_op jit(solution)/shard_map/psum | solution.py:41
  260.5 3.1 collective-permute-start.8
  269.3 7.3 %collective-permute-start.10 = (f32[96,32]{1,0:T(8,128)S(1)}, f32[96,32]{1,0:T(8,128)S(1)}, u32[]{:S(2)}, u32[]{:S(2)}) collective-permute-start(f32[96,32]{1,0:T(8,128)S(1)} %get-tuple-element.969), channel_id=1, source_target_pairs={{0,1},{1,2},{2,3},{3,4},{4,5},{5,6},{6,7},{8,9},{9,10},{10,11},{11... | collective-permute-start | bytes 36872 | tf_op jit(solution)/shard_map/ppermute | solution.py:15
  278.5 3.5 collective-permute-done.11
  282.1 24.5 %while.100 = (s32[]{:T(128)}, f32[32,256]{1,0:T(8,128)S(1)}, f32[65,65]{1,0:T(8,128)S(1)}, f32[96,320]{1,0:T(8,128)S(1)}, s32[]{:T(128)}, /*index=5*/s32[]{:T(12...) while((s32[]{:T(128)}, f32[32,256]{1,0:T(8,128)S(1)}, ...), condition=%wide.region_17.18_spmd.clone, body=%wide.region_16.17_spmd.clone.sunk | while | flops 47235088 | bytes 1324147 | solution.py:73
  307.9 10.7 %psum.98 = f32[3]{0:T(128)S(1)} all-reduce(f32[3]{0:T(128)S(1)} %convolution_bitcast_fusion.1), channel_id=1, replica_groups=mesh['gx'=4,'gy'=8] {'gy'}, use_global_device_ids=true, to_apply=%region_18.19 | all-reduce | flops 3 | bytes 24 | tf_op jit(solution)/shard_map/psum | solution.py:85
  319.2 5.5 psum.99
  325.8 43.5 %psum.100 = f32[]{:T(128)} all-reduce(f32[]{:T(128)} %multiply_reduce_fusion.1), channel_id=1, replica_groups=mesh['gx'=4,'gy'=8] {'gx','gy'}, use_global_device_ids=true, to_apply=%region_21.22 | all-reduce | flops 1 | bytes 8 | tf_op jit(solution)/shard_map/psum | solution.py:41
  378.9 7.1 %collective-permute-start.14 = (f32[96,32]{1,0:T(8,128)S(1)}, f32[96,32]{1,0:T(8,128)S(1)}, u32[]{:S(2)}, u32[]{:S(2)}) collective-permute-start(f32[96,32]{1,0:T(8,128)S(1)} %get-tuple-element.967), channel_id=1, source_target_pairs={{0,1},{1,2},{2,3},{3,4},{4,5},{5,6},{6,7},{8,9},{9,10},{10,11},{11... | collective-permute-start | bytes 36872 | tf_op jit(solution)/shard_map/ppermute | solution.py:15
  388.0 3.5 collective-permute-done.15
  391.6 24.5 %while.101 = (s32[]{:T(128)}, f32[32,256]{1,0:T(8,128)S(1)}, f32[65,65]{1,0:T(8,128)S(1)}, f32[96,320]{1,0:T(8,128)S(1)}, s32[]{:T(128)}, /*index=5*/s32[]{:T(12...) while((s32[]{:T(128)}, f32[32,256]{1,0:T(8,128)S(1)}, ...), condition=%wide.region_24.25_spmd.clone, body=%wide.region_23.24_spmd.clone.sunk | while | flops 47235088 | bytes 1324147 | solution.py:73
  418.7 10.8 %psum.101 = f32[4]{0:T(128)S(1)} all-reduce(f32[4]{0:T(128)S(1)} %convolution_bitcast_fusion), channel_id=1, replica_groups=mesh['gx'=4,'gy'=8] {'gy'}, use_global_device_ids=true, to_apply=%region_25.26 | all-reduce | flops 4 | bytes 32 | tf_op jit(solution)/shard_map/psum | solution.py:85
  430.9 6.2 %psum.102 = f32[4]{0:T(128)S(1)} all-reduce(f32[4]{0:T(128)S(1)} %psum.101), channel_id=1, replica_groups=mesh['gx'=4,'gy'=8] {'gx'}, use_global_device_ids=true, to_apply=%region_26.27 | all-reduce | flops 4 | bytes 32 | tf_op jit(solution)/shard_map/psum | solution.py:85
  438.2 42.8 %psum.103 = f32[]{:T(128)} all-reduce(f32[]{:T(128)} %fusion.60), channel_id=1, replica_groups=mesh['gx'=4,'gy'=8] {'gx','gy'}, use_global_device_ids=true, to_apply=%region_28.29 | all-reduce | flops 1 | bytes 8 | tf_op jit(solution)/shard_map/psum | solution.py:41
  508.7 3.4 collective-permute-done.17
  512.2 7.4 %collective-permute-start.18 = (f32[96,32]{1,0:T(8,128)S(1)}, f32[96,32]{1,0:T(8,128)S(1)}, u32[]{:S(2)}, u32[]{:S(2)}) collective-permute-start(f32[96,32]{1,0:T(8,128)S(1)} %get-tuple-element.965), channel_id=1, source_target_pairs={{0,1},{1,2},{2,3},{3,4},{4,5},{5,6},{6,7},{8,9},{9,10},{10,11},{11... | collective-permute-start | bytes 36872 | tf_op jit(solution)/shard_map/ppermute | solution.py:15
  521.6 3.5 collective-permute-done.19
  525.1 24.5 %while.102 = (s32[]{:T(128)}, f32[32,256]{1,0:T(8,128)S(1)}, f32[65,65]{1,0:T(8,128)S(1)}, f32[96,320]{1,0:T(8,128)S(1)}, s32[]{:T(128)}, /*index=5*/s32[]{:T(12...) while((s32[]{:T(128)}, f32[32,256]{1,0:T(8,128)S(1)}, ...), condition=%wide.region_32.33_spmd.clone, body=%wide.region_31.32_spmd.clone.sunk | while | flops 47235088 | bytes 1324147 | solution.py:73
  (894 shorter events, 175.9 us)
Async XLA Ops:
  0.6 42.1 %copy-start.1 = (f32[32,256]{1,0:T(8,128)S(1)}, f32[32,256]{1,0:T(8,128)}, u32[]{:S(2)}) copy-start(f32[32,256]{1,0:T(8,128)} %param.29) | copy-start | bytes 98308
  42.7 5.3 copy-start.5
  42.7 6.6 %collective-permute-start = (f32[32,256]{1,0:T(8,128)S(1)}, f32[32,256]{1,0:T(8,128)S(1)}, u32[]{:S(2)}, u32[]{:S(2)}) collective-permute-start(f32[32,256]{1,0:T(8,128)S(1)} %broadcast_divide_fusion.3), channel_id=1, source_target_pairs={{0,8},{8,16},{16,24},{1,9},{9,17},{17,25},{2,10},{10,18},{18,26},{... | collective-permute-start | bytes 98312 | tf_op jit(solution)/shard_map/ppermute | solution.py:15
  45.9 5.6 %collective-permute-start.1 = (f32[32,256]{1,0:T(8,128)S(1)}, f32[32,256]{1,0:T(8,128)S(1)}, u32[]{:S(2)}, u32[]{:S(2)}) collective-permute-start(f32[32,256]{1,0:T(8,128)S(1)} %broadcast_divide_fusion.3), channel_id=1, source_target_pairs={{8,0},{16,8},{24,16},{9,1},{17,9},{25,17},{10,2},{18,10},{26,18},{... | collective-permute-start | bytes 98312 | tf_op jit(solution)/shard_map/ppermute | solution.py:18
  48.1 0.7 copy-start.4
  51.5 9.5 %collective-permute-start.2 = (f32[96,32]{1,0:T(8,128)S(1)}, f32[96,32]{1,0:T(8,128)S(1)}, u32[]{:S(2)}, u32[]{:S(2)}) collective-permute-start(f32[96,32]{1,0:T(8,128)S(1)} %get-tuple-element.973), channel_id=1, source_target_pairs={{0,1},{1,2},{2,3},{3,4},{4,5},{5,6},{6,7},{8,9},{9,10},{10,11},{11... | collective-permute-start | bytes 36872 | tf_op jit(solution)/shard_map/ppermute | solution.py:15
  58.3 5.4 collective-permute-start.3
  61.0 2.9 copy-start
  63.9 24.5 %copy-start.2 = (f32[32,256]{1,0:T(8,128)S(1)}, f32[32,256]{1,0:T(8,128)}, u32[]{:S(2)}) copy-start(f32[32,256]{1,0:T(8,128)} %param.30) | copy-start | bytes 98308
  151.9 5.3 collective-permute-start.4
  155.0 5.6 %collective-permute-start.5 = (f32[32,256]{1,0:T(8,128)S(1)}, f32[32,256]{1,0:T(8,128)S(1)}, u32[]{:S(2)}, u32[]{:S(2)}) collective-permute-start(f32[32,256]{1,0:T(8,128)S(1)} %broadcast_divide_fusion.2), channel_id=1, source_target_pairs={{8,0},{16,8},{24,16},{9,1},{17,9},{25,17},{10,2},{18,10},{26,18},{... | collective-permute-start | bytes 98312 | tf_op jit(solution)/shard_map/ppermute | solution.py:18
  160.7 9.2 %collective-permute-start.6 = (f32[96,32]{1,0:T(8,128)S(1)}, f32[96,32]{1,0:T(8,128)S(1)}, u32[]{:S(2)}, u32[]{:S(2)}) collective-permute-start(f32[96,32]{1,0:T(8,128)S(1)} %get-tuple-element.971), channel_id=1, source_target_pairs={{0,1},{1,2},{2,3},{3,4},{4,5},{5,6},{6,7},{8,9},{9,10},{10,11},{11... | collective-permute-start | bytes 36872 | tf_op jit(solution)/shard_map/ppermute | solution.py:15
  167.9 5.4 collective-permute-start.7
  260.5 5.9 %collective-permute-start.8 = (f32[32,256]{1,0:T(8,128)S(1)}, f32[32,256]{1,0:T(8,128)S(1)}, u32[]{:S(2)}, u32[]{:S(2)}) collective-permute-start(f32[32,256]{1,0:T(8,128)S(1)} %broadcast_divide_fusion.1), channel_id=1, source_target_pairs={{0,8},{8,16},{16,24},{1,9},{9,17},{17,25},{2,10},{10,18},{18,26},{... | collective-permute-start | bytes 98312 | tf_op jit(solution)/shard_map/ppermute | solution.py:15
  263.6 5.6 %collective-permute-start.9 = (f32[32,256]{1,0:T(8,128)S(1)}, f32[32,256]{1,0:T(8,128)S(1)}, u32[]{:S(2)}, u32[]{:S(2)}) collective-permute-start(f32[32,256]{1,0:T(8,128)S(1)} %broadcast_divide_fusion.1), channel_id=1, source_target_pairs={{8,0},{16,8},{24,16},{9,1},{17,9},{25,17},{10,2},{18,10},{26,18},{... | collective-permute-start | bytes 98312 | tf_op jit(solution)/shard_map/ppermute | solution.py:18
  269.3 9.2 %collective-permute-start.10 = (f32[96,32]{1,0:T(8,128)S(1)}, f32[96,32]{1,0:T(8,128)S(1)}, u32[]{:S(2)}, u32[]{:S(2)}) collective-permute-start(f32[96,32]{1,0:T(8,128)S(1)} %get-tuple-element.969), channel_id=1, source_target_pairs={{0,1},{1,2},{2,3},{3,4},{4,5},{5,6},{6,7},{8,9},{9,10},{10,11},{11... | collective-permute-start | bytes 36872 | tf_op jit(solution)/shard_map/ppermute | solution.py:15
  276.5 5.4 collective-permute-start.11
  370.0 8.8 %collective-permute-start.12 = (f32[32,256]{1,0:T(8,128)S(1)}, f32[32,256]{1,0:T(8,128)S(1)}, u32[]{:S(2)}, u32[]{:S(2)}) collective-permute-start(f32[32,256]{1,0:T(8,128)S(1)} %broadcast_divide_fusion), channel_id=1, source_target_pairs={{0,8},{8,16},{16,24},{1,9},{9,17},{17,25},{2,10},{10,18},{18,26},{... | collective-permute-start | bytes 98312 | tf_op jit(solution)/shard_map/ppermute | solution.py:15
  373.1 5.7 %collective-permute-start.13 = (f32[32,256]{1,0:T(8,128)S(1)}, f32[32,256]{1,0:T(8,128)S(1)}, u32[]{:S(2)}, u32[]{:S(2)}) collective-permute-start(f32[32,256]{1,0:T(8,128)S(1)} %broadcast_divide_fusion), channel_id=1, source_target_pairs={{8,0},{16,8},{24,16},{9,1},{17,9},{25,17},{10,2},{18,10},{26,18},{... | collective-permute-start | bytes 98312 | tf_op jit(solution)/shard_map/ppermute | solution.py:18
  378.9 9.1 %collective-permute-start.14 = (f32[96,32]{1,0:T(8,128)S(1)}, f32[96,32]{1,0:T(8,128)S(1)}, u32[]{:S(2)}, u32[]{:S(2)}) collective-permute-start(f32[96,32]{1,0:T(8,128)S(1)} %get-tuple-element.967), channel_id=1, source_target_pairs={{0,1},{1,2},{2,3},{3,4},{4,5},{5,6},{6,7},{8,9},{9,10},{10,11},{11... | collective-permute-start | bytes 36872 | tf_op jit(solution)/shard_map/ppermute | solution.py:15
  386.0 5.4 collective-permute-start.15
  503.4 46.2 %copy-start.3 = (f32[32,256]{1,0:T(8,128)}, f32[32,256]{1,0:T(8,128)S(1)}, u32[]{:S(2)}) copy-start(f32[32,256]{1,0:T(8,128)S(1)} %multiply_add_fusion) | copy-start | bytes 98308
  503.4 5.3 collective-permute-start.16
  506.5 5.6 %collective-permute-start.17 = (f32[32,256]{1,0:T(8,128)S(1)}, f32[32,256]{1,0:T(8,128)S(1)}, u32[]{:S(2)}, u32[]{:S(2)}) collective-permute-start(f32[32,256]{1,0:T(8,128)S(1)} %multiply_add_fusion), channel_id=1, source_target_pairs={{8,0},{16,8},{24,16},{9,1},{17,9},{25,17},{10,2},{18,10},{26,18},{... | collective-permute-start | bytes 98312 | tf_op jit(solution)/shard_map/ppermute | solution.py:18
  512.2 9.4 %collective-permute-start.18 = (f32[96,32]{1,0:T(8,128)S(1)}, f32[96,32]{1,0:T(8,128)S(1)}, u32[]{:S(2)}, u32[]{:S(2)}) collective-permute-start(f32[96,32]{1,0:T(8,128)S(1)} %get-tuple-element.965), channel_id=1, source_target_pairs={{0,1},{1,2},{2,3},{3,4},{4,5},{5,6},{6,7},{8,9},{9,10},{10,11},{11... | collective-permute-start | bytes 36872 | tf_op jit(solution)/shard_map/ppermute | solution.py:15
  519.6 5.4 collective-permute-start.19
